TPU v7x, 32 devices: a whole 2x2x4 slice. The times are simulated.
32 devices in a mesh: rows: 16 (over z, y, x), feat: 2 (over core).
Axes of the slice: x: 2, y: 2, z: 4, core: 2. Of those that a mesh axis runs over, the one named last changes fastest.
Arguments:
- queries: bfloat16 [1024, 128], P('rows', 'feat'), may hold values from -6 to 6
- corpus: bfloat16 [524288, 128], P(('rows', 'feat')), as said below
- candidates: int32 [1024, 100], P(('rows', 'feat')), may hold values from 0 to 524287, as said below
- threshold: int32 [1024], replicated, may hold values from 100 to 199, as said below
Outputs:
- exceed: float32 [1024], P(('rows', 'feat'))
- candidate_scores: float32 [1024, 100], P(('rows', 'feat'))
Inputs may be any that keep to these rules, and one draw needn't show every extreme that they name: Passage ids. Of the 3200 candidates of one device's queries (aligned blocks of 32 rows), at most 100 lie in the 16384 passages of any one device, and exactly 100 in some device's. `corpus`: passage embeddings of order one or smaller; their scale differs between passages. Some query has threshold 100 and some 199.
All inputs are finite; a program needn't handle non-finite values.
Results may differ from a plain program's by a relative error of at most 0.00035.
Values may be sent and summed in bfloat16 or wider, within the bound.
A program may use at most 64 MiB of HBM per device.

v0:
```python
import functools

import jax
import jax.numpy as jnp
from jax import lax
from jax.experimental import pallas as pl
from jax.experimental.pallas import tpu as pltpu
from jax.sharding import PartitionSpec as P

LANES = 128
TILE = 256
BLOCK = 4096
MIXED = 2048
STEP = 512
MESH = pl.DeviceIdType.MESH


def bulk_wait(ref, sem):
    pltpu.make_async_copy(ref, ref, sem).wait()


def kernel(
    n, nf, npass_all, capacity,
    q_hbm, thr_hbm, cand_hbm, corpus_ref,
    mass_out, ans_out,
    q_ref, thr_ref, cand_ref, corpus_v, corpus_f, q_pack, q_in, q_full, q_turned, cand_pad, places,
    ids_out, ids_in, ids_at, ids_sm, rows_v, vals_out, vals_in, mass_rows, mass_in,
    small_sem, load_sem, sm_sem, q_send, q_recv, hand_send, hand_recv, far_sem, ids_send, ids_recv, vals_send, vals_recv, mass_send, mass_recv,
):
    rows_dev, width = corpus_v.shape
    owned, per_query = cand_ref.shape
    nq = q_full.shape[0]
    half = q_ref.shape[1]
    tiles = nq // TILE
    dpt = TILE // owned
    chips = n // nf
    dpc = dpt // nf
    core = lax.axis_index("feat")
    me = lax.axis_index("rows") * nf + core
    my_tile = me // dpt
    my_j = me % dpt
    id_bits = rows_dev.bit_length() - 1
    beside = my_tile + 1 - 2 * (my_tile % 2)
    order = [beside]
    for k in range(1, tiles // 2):
        order += [(my_tile + 2 * k) % tiles, (beside + 2 * k) % tiles]
    order.append(my_tile)

    load = pltpu.make_async_copy(corpus_ref, corpus_v, load_sem)
    small = [
        pltpu.make_async_copy(src, dst, small_sem.at[k])
        for k, (src, dst) in enumerate(((q_hbm, q_ref), (cand_hbm, cand_ref), (thr_hbm, thr_ref)))]
    for copy in small:
        copy.start()
    load.start()

    def peers(i, act):
        def step(j, carry):
            act(order[i] * dpt + (my_j + j) % dpt)
            return carry
        lax.fori_loop(1 if i == tiles - 1 else 0, dpt, step, 0, unroll=True)

    def where_is(d):
        return (d // nf, d % nf)

    barrier = pltpu.get_barrier_semaphore()
    inner = (my_tile >= 1) & (my_tile < tiles - 1)
    across = (tiles - 1 - my_tile) * dpt + my_j
    nearby = beside * dpt + my_j

    def signal(sem, d):
        pl.semaphore_signal(sem, inc=1, device_id=where_is(d), device_id_type=MESH)

    @pl.when(inner)
    def _():
        signal(barrier, across)
    peers(0, functools.partial(signal, barrier))
    peers(tiles - 1, functools.partial(signal, barrier))

    for copy in small:
        copy.wait()
    q_local = q_ref[...].astype(jnp.float32)
    mine = jnp.concatenate([q_local[:owned], q_local[owned:]], axis=1).astype(jnp.bfloat16)
    q_pack[...] = mine
    my_place = core * chips + me // nf
    q_in[my_place] = mine

    cand_pad[...] = jnp.full(cand_pad.shape, -1, jnp.int32)
    cand_pad[:, :per_query] = cand_ref[...]
    cand = cand_pad[...]
    target = lax.shift_right_arithmetic(cand, jnp.int32(id_bits))
    local = jnp.bitwise_and(cand, jnp.int32(rows_dev - 1))
    low = jnp.bitwise_and(local, jnp.int32(LANES - 1)).astype(jnp.float32)
    high = lax.shift_right_arithmetic(local, jnp.int32(7)).astype(jnp.float32)
    dest = lax.broadcasted_iota(jnp.int32, (n, LANES), 0)
    hot = [jnp.where(target[q:q + 1] == dest, 1.0, 0.0) for q in range(owned)]
    row_i = lax.broadcasted_iota(jnp.int32, (LANES, 2 * LANES), 0)
    col_i = lax.broadcasted_iota(jnp.int32, (LANES, 2 * LANES), 1)
    upper = jnp.where((row_i < col_i) | (col_i >= LANES), 1.0, 0.0).astype(jnp.bfloat16)
    counts = jnp.dot(
        jnp.concatenate(hot, axis=0).astype(jnp.bfloat16), upper, preferred_element_type=jnp.float32)
    base = jnp.zeros((n, LANES), jnp.float32)
    slot = lax.broadcasted_iota(jnp.int32, (LANES, LANES), 0).astype(jnp.float32)
    fields = []
    for q in range(owned):
        block = counts[q * n:(q + 1) * n]
        rank = jnp.sum(hot[q] * (block[:, :LANES] + base), axis=0, keepdims=True)
        base = base + block[:, LANES:]
        places[:, q * LANES:(q + 1) * LANES] = jnp.where(rank == slot, 1.0, 0.0).astype(jnp.bfloat16)
        fields.append(jnp.concatenate(
            [hot[q] * low[q:q + 1], hot[q] * high[q:q + 1], hot[q] * float(q)], axis=0
        ).astype(jnp.bfloat16))
    sorted_fields = lax.dot_general(
        jnp.concatenate(fields, axis=1), places[...], (((1,), (1,)), ((), ())),
        preferred_element_type=jnp.float32)
    packed = (
        sorted_fields[:n] + sorted_fields[n:2 * n] * float(LANES) + sorted_fields[2 * n:] * float(rows_dev)
    ).astype(jnp.int32)
    for t in range(n):
        ids_out[t] = packed[t:t + 1]

    load.wait()

    def widen(b, carry):
        at = pl.ds(pl.multiple_of(b * STEP, STEP), STEP)
        corpus_f[at, :] = corpus_v[at, :].astype(jnp.float32)
        return carry
    lax.fori_loop(0, rows_dev // STEP, widen, 0)

    @pl.when(inner)
    def _():
        pl.semaphore_wait(barrier, 2 * dpt)

    @pl.when(jnp.logical_not(inner))
    def _():
        pl.semaphore_wait(barrier, 2 * dpt - 1)

    def send_queries(d):
        pltpu.make_async_remote_copy(
            src_ref=q_pack, dst_ref=q_in.at[my_place], send_sem=q_send, recv_sem=q_recv.at[my_tile],
            device_id=where_is(d), device_id_type=MESH).start()

    def send_ids(d):
        pltpu.make_async_remote_copy(
            src_ref=ids_out.at[d], dst_ref=ids_in.at[me], send_sem=ids_send, recv_sem=ids_recv,
            device_id=where_is(d), device_id_type=MESH).start()

    @pl.when(inner)
    def _():
        signal(far_sem, across)
    peers(0, send_queries)
    peers(tiles - 1, send_queries)
    peers(0, send_ids)
    peers(tiles - 1, send_ids)
    pl.semaphore_wait(far_sem, 1)

    @pl.when(inner)
    def _():
        signal(far_sem, nearby)
    for i in range(1, tiles - 1):
        peers(i, send_ids)
    for i in range(1, tiles - 1):
        for j in range(dpc):
            send_queries((order[i] * dpc + (my_j // nf + j) % dpc) * nf + core)
    ids_in[me] = ids_out[me]

    def hand_over(i):
        blocks_of = q_in.at[pl.ds(core * chips + order[i] * dpc, dpc)]
        bulk_wait(q_in.at[pl.ds(0, dpc)], q_recv.at[order[i]])
        pltpu.make_async_remote_copy(
            src_ref=blocks_of, dst_ref=blocks_of, send_sem=hand_send, recv_sem=hand_recv.at[order[i]],
            device_id=where_is(me + 1 - 2 * core), device_id_type=MESH).start()

    def unpack(i):
        if i == 0:
            bulk_wait(q_in.at[pl.ds(0, dpt)], q_recv.at[order[i]])
        elif i == tiles - 1:
            bulk_wait(q_in.at[pl.ds(0, dpt - 1)], q_recv.at[order[i]])
        else:
            bulk_wait(q_in.at[pl.ds(0, dpc)], hand_recv.at[order[i]])
        parts = []
        for g in range(dpc):
            f0 = q_in[order[i] * dpc + g].astype(jnp.float32)
            f1 = q_in[chips + order[i] * dpc + g].astype(jnp.float32)
            parts.append(jnp.where(left, f0, pltpu.roll(f1, half, 1)))
            parts.append(jnp.where(left, pltpu.roll(f0, half, 1), f1))
        asked = jnp.concatenate(parts, axis=0)
        q_full[pl.ds(pl.multiple_of(order[i] * TILE, TILE), TILE), :] = asked.astype(jnp.bfloat16)
        q_turned[order[i]] = asked.T.astype(jnp.bfloat16)

    left = lax.broadcasted_iota(jnp.int32, (owned, LANES), 1) < half
    to_smem = pltpu.make_async_copy(ids_at, ids_sm, sm_sem)
    gather_tile = tiles - 2
    part = n // (rows_dev // MIXED)

    def collect(source):
        for r in range(capacity):
            rows_v[source, pl.ds(r, 1), :] = corpus_f[pl.ds(ids_sm[source, 0, r], 1), :]

    def answer(source):
        pairs = lax.dot_general(
            q_full[pl.ds(pl.multiple_of(source * owned, owned), owned), :],
            rows_v[source].astype(jnp.bfloat16),
            (((1,), (1,)), ((), ())), preferred_element_type=jnp.float32)
        who = lax.shift_right_arithmetic(ids_in[source], jnp.int32(id_bits))
        mask = (who == lax.broadcasted_iota(jnp.int32, (owned, LANES), 0)) & (
            lax.broadcasted_iota(jnp.int32, (owned, LANES), 1) < capacity)
        vals_out[source] = jnp.sum(jnp.where(mask, pairs, 0.0), axis=0, keepdims=True)

    unpack(tiles - 1)
    for i in range(tiles):
        tile = order[i]
        if i < tiles - 1:
            unpack(i)
        size = MIXED if i == gather_tile else BLOCK
        blocks = rows_dev // size
        cutoff = thr_ref[:, pl.ds(pl.multiple_of(tile * TILE, TILE), TILE)].astype(jnp.float32) * 0.01
        if i == gather_tile:
            to_smem.wait()

        def sweep(b, acc):
            weights = q_turned[tile]
            sums = []
            for h in range(2):
                at = pl.ds(pl.multiple_of(b * size + h * (size // 2), size // 2), size // 2)
                scores = jnp.dot(corpus_v[at, :], weights, preferred_element_type=jnp.float32)
                over = jnp.maximum(scores - cutoff, 0.0).reshape(size // 32, 2, 8, TILE)
                sums.append(jnp.sum(over, axis=0))
            if i == gather_tile:
                for k in range(part):
                    collect(b * part + k)
                    answer(jnp.maximum(b - 1, 0) * part + k)
            return acc[0] + sums[0], acc[1] + sums[1]

        zero = jnp.zeros((2, 8, TILE), jnp.float32)
        acc = lax.fori_loop(0, blocks // 2, sweep, (zero, zero))
        if i + 1 < tiles - 1:
            hand_over(i + 1)
        if i == gather_tile - 1:
            bulk_wait(ids_in.at[pl.ds(0, n - 1)], ids_recv)
            ids_at[...] = jnp.bitwise_and(ids_in[...], jnp.int32(rows_dev - 1))
            to_smem.start()
        acc = lax.fori_loop(blocks // 2, blocks, sweep, acc)
        acc = acc[0] + acc[1]
        acc = acc[0] + acc[1]
        total = jnp.sum(acc, axis=0, keepdims=True)
        for h in range(TILE // LANES):
            mass_rows[tile * (TILE // LANES) + h] = total[:, h * LANES:(h + 1) * LANES]

        def send_mass(d):
            pltpu.make_async_remote_copy(
                src_ref=mass_rows.at[d * owned // LANES], dst_ref=mass_in.at[me],
                send_sem=mass_send, recv_sem=mass_recv,
                device_id=where_is(d), device_id_type=MESH).start()
        peers(i, send_mass)
        if i == tiles - 1:
            mass_in[me] = mass_rows[me * owned // LANES]

        if i == gather_tile:
            for k in range(part):
                answer(n - part + k)

            def send_vals(d):
                pltpu.make_async_remote_copy(
                    src_ref=vals_out.at[d], dst_ref=vals_in.at[me], send_sem=vals_send, recv_sem=vals_recv,
                    device_id=where_is(d), device_id_type=MESH).start()
            for u in range(tiles):
                peers(u, send_vals)
            vals_in[me] = vals_out[me]

    bulk_wait(vals_in.at[pl.ds(0, n - 1)], vals_recv)
    values = jnp.concatenate([vals_in[t] for t in range(n)], axis=0)
    top = values.astype(jnp.bfloat16)
    rest = values - top.astype(jnp.float32)
    mid = rest.astype(jnp.bfloat16)
    last = (rest - mid.astype(jnp.float32)).astype(jnp.bfloat16)
    pieces = jnp.concatenate([top, mid, last], axis=0)
    cand = cand_pad[...]
    target = lax.shift_right_arithmetic(cand, jnp.int32(id_bits))
    for q in range(owned):
        spread = jnp.dot(
            pieces, places[:, q * LANES:(q + 1) * LANES], preferred_element_type=jnp.float32)
        spread = (spread[2 * n:] + spread[n:2 * n]) + spread[:n]
        ans_out[q:q + 1, :] = jnp.sum(
            jnp.where(target[q:q + 1] == dest, spread, 0.0), axis=0, keepdims=True)

    bulk_wait(mass_in.at[pl.ds(0, n - 1)], mass_recv)
    mass = mass_in[0]
    for t in range(1, n):
        mass = mass + mass_in[t]
    mass = mass * (8.0 / npass_all)
    per_row = LANES // owned
    result = mass
    for u in range(1, per_row):
        result = jnp.where(me % per_row == u, pltpu.roll(mass, LANES - u * owned, 1), result)
    mass_out[...] = result

    bulk_wait(q_in.at[pl.ds(0, 2 * dpt - 1 + (tiles - 2) * dpc)], q_send)
    bulk_wait(q_in.at[pl.ds(0, (tiles - 2) * dpc)], hand_send)
    bulk_wait(ids_in.at[pl.ds(0, n - 1)], ids_send)
    bulk_wait(vals_in.at[pl.ds(0, n - 1)], vals_send)
    bulk_wait(mass_in.at[pl.ds(0, n - 1)], mass_send)


def fused_body(n, nf, queries, corpus, candidates, threshold):
    rows_dev, width = corpus.shape
    owned, per_query = candidates.shape
    nq = n * owned
    capacity = (owned * per_query + n - 1) // n
    vmem = pl.BlockSpec(memory_space=pltpu.VMEM)
    mass, answers = pl.pallas_call(
        functools.partial(kernel, n, nf, rows_dev * n, capacity),
        out_shape=(
            jax.ShapeDtypeStruct((1, LANES), jnp.float32),
            jax.ShapeDtypeStruct((owned, LANES), jnp.float32),
        ),
        in_specs=[pl.BlockSpec(memory_space=pl.ANY)] * 4,
        out_specs=(vmem, vmem),
        scratch_shapes=[
            pltpu.VMEM(queries.shape, jnp.bfloat16),
            pltpu.VMEM((1, nq), jnp.int32),
            pltpu.VMEM((owned, per_query), jnp.int32),
            pltpu.VMEM((rows_dev, width), jnp.bfloat16),
            pltpu.VMEM((rows_dev, width), jnp.float32),
            pltpu.VMEM((owned, LANES), jnp.bfloat16),
            pltpu.VMEM((n, owned, LANES), jnp.bfloat16),
            pltpu.VMEM((nq, LANES), jnp.bfloat16),
            pltpu.VMEM((nq // TILE, LANES, TILE), jnp.bfloat16),
            pltpu.VMEM((owned, LANES), jnp.int32),
            pltpu.VMEM((LANES, owned * LANES), jnp.bfloat16),
            pltpu.VMEM((n, 1, LANES), jnp.int32),
            pltpu.VMEM((n, 1, LANES), jnp.int32),
            pltpu.VMEM((n, 1, LANES), jnp.int32),
            pltpu.SMEM((n, 1, LANES), jnp.int32),
            pltpu.VMEM((n, LANES, LANES), jnp.float32),
            pltpu.VMEM((n, 1, LANES), jnp.float32),
            pltpu.VMEM((n, 1, LANES), jnp.float32),
            pltpu.VMEM((nq // LANES, 1, LANES), jnp.float32),
            pltpu.VMEM((n, 1, LANES), jnp.float32),
            pltpu.SemaphoreType.DMA((3,)),
            pltpu.SemaphoreType.DMA,
            pltpu.SemaphoreType.DMA,
            pltpu.SemaphoreType.DMA,
            pltpu.SemaphoreType.DMA((nq // TILE,)),
            pltpu.SemaphoreType.DMA,
            pltpu.SemaphoreType.DMA((nq // TILE,)),
            pltpu.SemaphoreType.REGULAR,
            pltpu.SemaphoreType.DMA,
            pltpu.SemaphoreType.DMA,
            pltpu.SemaphoreType.DMA,
            pltpu.SemaphoreType.DMA,
            pltpu.SemaphoreType.DMA,
            pltpu.SemaphoreType.DMA,
        ],
        compiler_params=pltpu.CompilerParams(
            collective_id=0, has_side_effects=True),
    )(queries, threshold.reshape(1, nq), candidates, corpus)
    return mass[0, :owned], answers[:, :per_query]


def plain_body(queries, corpus, candidates, threshold):
    rows_dev = corpus.shape[0]
    width = corpus.shape[1]
    shards = lax.axis_size("rows") * lax.axis_size("feat")
    owned_queries = candidates.shape[0]
    per_query = candidates.shape[1]
    npass_all = rows_dev * shards
    cutoff = threshold.astype(jnp.float32) * 0.01
    owner = lax.axis_index(("rows", "feat"))
    full_rows = lax.all_gather(queries, "feat", axis=1, tiled=True)
    whole = lax.all_gather(full_rows, "rows", axis=0, tiled=True)
    query_count = whole.shape[0]
    block = 2048
    corpus_blocks = corpus.reshape(rows_dev // block, block, width)

    def visit(total, block_rows):
        scores = lax.dot_general(
            whole, block_rows, (((1,), (1,)), ((), ())), preferred_element_type=jnp.float32
        )
        return (total + jnp.sum(jnp.maximum(scores - cutoff[:, None], 0.0), axis=1), None)

    total, _ = lax.scan(visit, jnp.zeros((query_count,), jnp.float32), corpus_blocks)
    flat_ids = candidates.reshape(-1)
    total_ids = flat_ids.shape[0]
    capacity = (total_ids + shards - 1) // shards
    target = flat_ids // rows_dev
    onehot = (target[:, None] == jnp.arange(shards, dtype=jnp.int32)[None, :]).astype(jnp.int32)
    before = jnp.cumsum(onehot, axis=0) - onehot
    rank = jnp.sum(before * onehot, axis=1)
    query_ids = owner * owned_queries + jnp.arange(total_ids, dtype=jnp.int32) // per_query
    fields = jnp.stack([flat_ids - target * rows_dev, query_ids], axis=1)
    send_both = jnp.zeros((shards, capacity, 2), jnp.int32).at[target, rank].set(fields)
    n_rows = lax.axis_size("rows")
    n_feat = lax.axis_size("feat")
    received = lax.all_to_all(
        lax.all_to_all(
            send_both.reshape(n_rows, n_feat, capacity * 2),
            "rows",
            split_axis=0,
            concat_axis=0,
            tiled=True,
        ),
        "feat",
        split_axis=1,
        concat_axis=1,
        tiled=True,
    )
    received = received.reshape(shards * capacity, 2)
    picked = corpus[received[:, 0]]
    asked = whole[received[:, 1]]
    values = jnp.einsum("kd,kd->k", picked, asked, preferred_element_type=jnp.float32).reshape(
        n_rows, n_feat, capacity
    )
    partials = total.reshape(n_rows, n_feat, owned_queries)
    answers, mass_parts = (
        lax.all_to_all(
            lax.all_to_all(values, "rows", split_axis=0, concat_axis=0, tiled=True),
            "feat",
            split_axis=1,
            concat_axis=1,
            tiled=True,
        ),
        lax.all_to_all(
            lax.all_to_all(partials, "rows", split_axis=0, concat_axis=0, tiled=True),
            "feat",
            split_axis=1,
            concat_axis=1,
            tiled=True,
        ),
    )
    exceed = jnp.sum(mass_parts, axis=(0, 1)) * (8.0 / npass_all)
    candidate_scores = answers.reshape(shards, capacity)[target, rank].reshape(
        owned_queries, per_query
    )
    return (exceed, candidate_scores)


def body(queries, corpus, candidates, threshold):
    nf = lax.axis_size("feat")
    n = lax.axis_size("rows") * nf
    rows_dev, width = corpus.shape
    owned, per_query = candidates.shape
    capacity = (owned * per_query + n - 1) // n
    fits = (
        nf == 2
        and width == LANES
        and queries.shape == (2 * owned, LANES // 2)
        and owned % 32 == 0
        and LANES % owned == 0
        and per_query <= LANES
        and capacity <= LANES
        and n % 8 == 0
        and (n * owned) % TILE == 0
        and n * owned == 4 * TILE
        and rows_dev % BLOCK == 0
        and n % (rows_dev // MIXED) == 0
        and rows_dev % (2 * BLOCK) == 0
        and rows_dev & (rows_dev - 1) == 0
    )
    if fits:
        return fused_body(n, nf, queries, corpus, candidates, threshold)
    return plain_body(queries, corpus, candidates, threshold)


def solution(mesh):
    return jax.shard_map(
        body,
        mesh=mesh,
        in_specs=(P("rows", "feat"), P(("rows", "feat"), None), P(("rows", "feat"), None), P()),
        out_specs=(P(("rows", "feat")), P(("rows", "feat"), None)),
        check_vma=False,
    )
```

profile of v0, /device:TPU:0, one launch (start us, length us, event | category | flops | bytes accessed | tf_op | source)
XLA Modules:
  0.0 31.0 jit_solution(425735622585640767)
XLA Ops:
  0.6 27.9 %shard_map.59 = (f32[1,128]{1,0:T(1,128)}, f32[32,128]{1,0:T(8,128)}) custom-call(bf16[64,64]{1,0:T(8,128)(2,1)} %q_hbm.1, s32[1,1024]{1,0:T(1,128)} %bitcast.5, s32[32,100]{1,0:T(8,128)} %cand_hbm.1, bf16[16384,128]{1,0:T(8,128)(2,1)} %corpus_ref.1), custom_call_target="tpu_custom_call" | custom-call | tf_op jit(solution)/shard_map/pallas_call | solution.py:311
  28.5 1.1 %slice_bitcast_fusion = f32[32]{0:T(128)} fusion(f32[1,128]{1,0:T(1,128)} %get-tuple-element.4), kind=kLoop, calls=%fused_computation | loop fusion | bytes 256 | tf_op jit(solution)/shard_map/squeeze | solution.py:358
  29.7 1.3 %copy.7 = f32[32,100]{1,0:T(8,128)} copy(f32[32,100]{1,0:T(8,128)} %bitcast.4) | data formatting | bytes 25600
where the time goes:
time: 31.3 us; the launch traced here: 31 us
  Pallas kernels  27.9 us (89%)
  local copies, waits for them, and re-layouts  2.46 us (8%)
  between operations  0.64 us (2%)
    pallas_call x1, Pallas kernels, fused_body(): pl.pallas_call(functools.partial(kernel, n, nf, rows_dev * n, capacity),...  27.9 us
    unnamed x1, local copies, waits for them, and re-layouts  1.32 us
    squeeze x1, local copies, waits for them, and re-layouts, fused_body(): return (mass[0, :owned], answers[:, :per_query])  1.14 us

commit v1 on v0

v1 whole, which is shorter than its diff:
```python
import functools

import jax
import jax.numpy as jnp
from jax import lax
from jax.experimental import pallas as pl
from jax.experimental.pallas import tpu as pltpu
from jax.sharding import PartitionSpec as P

LANES = 128
TILE = 256
ROWS = 256
PIECES = 32
RANGES = 3
LAG = 2
UNITS = (88, 120, 152, 184)
PLAN = {
    0: (("reach", 1),), 40: (("reach", 2),), 48: (("hand", 1),), 72: (("reach", 3),), 96: (("hand", 2),),
    124: (("hand", 3),),
    70: (("ids", 0),), 84: (("sm", 0),), 104: (("ids", 1),), 118: (("sm", 1),),
    136: (("ids", 2),), 150: (("sm", 2),), 168: (("ids", 3),), 182: (("sm", 3),),
    134: (("vals", 0),), 166: (("vals", 1),), 198: (("vals", 2),), 230: (("vals", 3),),
}
MESH = pl.DeviceIdType.MESH


def mark(name):
    pass


def bulk_wait(ref, sem):
    pltpu.make_async_copy(ref, ref, sem).wait()


def kernel(
    n, nf, npass_all, capacity,
    q_hbm, thr_hbm, cand_hbm, corpus_ref,
    mass_hbm, ans_hbm,
    mass_out, ans_out,
    q_ref, thr_ref, cand_ref, corpus_v, corpus_f, q_pack, q_in, q_full, cand_pad, places,
    ids_out, ids_in, ids_at, ids_sm, rows_v, vals_out, vals_in, mass_rows, mass_in,
    small_sem, load_sem, out_sem, sm_sem, in_sem, q_send, q_recv, hand_send, hand_recv,
    ids_send, ids_recv, vals_send, vals_recv, mass_send, mass_recv,
):
    rows_dev, width = corpus_v.shape
    owned, per_query = cand_ref.shape
    nq = q_full.shape[0]
    half = q_ref.shape[1]
    tiles = nq // TILE
    dpt = TILE // owned
    dph = dpt // 2
    chips = n // nf
    dpc = dpt // nf
    core = lax.axis_index("feat")
    me = lax.axis_index("rows") * nf + core
    my_tile = me // dpt
    my_j = me % dpt
    my_half = my_j // dph
    my_h = my_j % dph
    id_bits = rows_dev.bit_length() - 1

    def table(values):
        out = values[0]
        for k in range(1, tiles):
            out = out + (values[k] - values[k - 1]) * ((my_tile + tiles - 1 - k) // (tiles - 1))
        return out

    planes = [my_tile, table((1, 0, 1, 2)), table((2, 2, 0, 1)), table((3, 3, 3, 0))]
    askers = [my_tile, table((1, 0, 1, 2)), table((2, 2, 0, 0)), table((3, 3, 3, 1))]

    load = pltpu.make_async_copy(corpus_ref, corpus_v, load_sem)
    small = [
        pltpu.make_async_copy(src, dst, small_sem.at[k])
        for k, (src, dst) in enumerate(((q_hbm, q_ref), (cand_hbm, cand_ref), (thr_hbm, thr_ref)))]
    for copy in small:
        copy.start()
    load.start()

    def where_is(d):
        return (d // nf, d % nf)

    own_half = [my_tile * dpt + my_half * dph + (my_h + i) % dph for i in range(1, dph)]
    other_half = [my_tile * dpt + (1 - my_half) * dph + (my_h + i) % dph for i in range(dph)]
    neighbours = own_half + other_half

    def plane_of(t):
        return [t * dpt + (my_j + j) % dpt for j in range(dpt)]

    def same_core_of(t):
        return [(t * dpc + (my_j // nf + j) % dpc) * nf + core for j in range(dpc)]

    barrier = pltpu.get_barrier_semaphore()

    def signal(sem, d):
        pl.semaphore_signal(sem, inc=1, device_id=where_is(d), device_id_type=MESH)

    mark("start")
    for d in neighbours:
        signal(barrier, d)
    for k in range(1, tiles):
        @pl.when(my_tile + k < tiles)
        def _():
            for d in plane_of(my_tile + k):
                signal(barrier, d)

    mark("smallwait")
    for copy in small:
        copy.wait()
    mark("pack")
    q_local = q_ref[...].astype(jnp.float32)
    mine = jnp.concatenate([q_local[:owned], q_local[owned:]], axis=1).astype(jnp.bfloat16)
    q_pack[...] = mine
    my_place = core * chips + me // nf
    q_in[my_place] = mine

    mark("barrier")
    pl.semaphore_wait(barrier, dpt - 1 + my_tile * dpt)
    mark("sends1")

    def send_queries(d, sem):
        pltpu.make_async_remote_copy(
            src_ref=q_pack, dst_ref=q_in.at[my_place], send_sem=q_send, recv_sem=sem,
            device_id=where_is(d), device_id_type=MESH).start()

    def send_ids(d):
        pltpu.make_async_remote_copy(
            src_ref=ids_out.at[d], dst_ref=ids_in.at[me], send_sem=ids_send, recv_sem=ids_recv.at[my_tile],
            device_id=where_is(d), device_id_type=MESH).start()

    for d in own_half:
        send_queries(d, q_recv.at[tiles])
    for d in other_half:
        send_queries(d, q_recv.at[tiles + 1])
    for k in range(1, tiles):
        @pl.when(my_tile >= k)
        def _():
            signal(in_sem.at[my_tile], me - k * dpt)
            for d in same_core_of(my_tile - k):
                send_queries(d, q_recv.at[my_tile])

    mark("sort")
    cand_pad[...] = jnp.full(cand_pad.shape, -1, jnp.int32)
    cand_pad[:, :per_query] = cand_ref[...]
    cand = cand_pad[...]
    target = lax.shift_right_arithmetic(cand, jnp.int32(id_bits))
    local = jnp.bitwise_and(cand, jnp.int32(rows_dev - 1))
    low = jnp.bitwise_and(local, jnp.int32(LANES - 1)).astype(jnp.float32)
    high = lax.shift_right_arithmetic(local, jnp.int32(7)).astype(jnp.float32)
    dest = lax.broadcasted_iota(jnp.int32, (n, LANES), 0)
    hot = [jnp.where(target[q:q + 1] == dest, 1.0, 0.0) for q in range(owned)]
    row_i = lax.broadcasted_iota(jnp.int32, (LANES, 2 * LANES), 0)
    col_i = lax.broadcasted_iota(jnp.int32, (LANES, 2 * LANES), 1)
    upper = jnp.where((row_i < col_i) | (col_i >= LANES), 1.0, 0.0).astype(jnp.bfloat16)

    def sort(count0, count1, field0, field1):
        blank = jnp.zeros((TILE, LANES), jnp.bfloat16)
        chunk = TILE // n
        refs = (count0, count1)
        for m in range(2):
            pltpu.matmul_push_rhs(
                jnp.concatenate([upper, jnp.zeros_like(upper)], axis=0), staging_register=0, mxu_index=m)
        for i in range(owned // chunk):
            part = jnp.concatenate(hot[i * chunk:(i + 1) * chunk], axis=0).astype(jnp.bfloat16)
            pltpu.matmul_acc_lhs(
                refs[i % 2][i // 2], jnp.concatenate([part, blank], axis=1),
                load_staged_rhs=0 if i < 2 else None)
        base = jnp.zeros((n, LANES), jnp.float32)
        slot = lax.broadcasted_iota(jnp.int32, (LANES, LANES), 0).astype(jnp.float32)
        fields = []
        for q in range(owned):
            if q % chunk == 0:
                counts = pltpu.matmul_pop(refs[q // chunk % 2][q // chunk // 2])
            block = counts[q % chunk * n:(q % chunk + 1) * n]
            rank = jnp.sum(hot[q] * (block[:, :LANES] + base), axis=0, keepdims=True)
            base = base + block[:, LANES:]
            places[:, q * LANES:(q + 1) * LANES] = jnp.where(rank == slot, 1.0, 0.0).astype(jnp.bfloat16)
            fields.append(jnp.concatenate(
                [hot[q] * low[q:q + 1], hot[q] * high[q:q + 1], hot[q] * float(q)], axis=0
            ).astype(jnp.bfloat16))
        sums = (field0, field1)
        turns = owned // 4
        for i in range(turns):
            pairs = (2 * i, owned // 2 + 2 * i)
            pltpu.matmul_push_rhs(
                jnp.concatenate([places[:, q * LANES:(q + 2) * LANES] for q in pairs], axis=0),
                staging_register=i // 2 % 2, mxu_index=i % 2, transpose=True)
            pltpu.matmul_acc_lhs(
                sums[i % 2],
                jnp.concatenate([jnp.concatenate(fields[q:q + 2], axis=1) for q in pairs], axis=0),
                load_staged_rhs=i // 2 % 2)
        total = pltpu.matmul_pop(field0) + pltpu.matmul_pop(field1)
        sorted_fields = total[:3 * n, :LANES] + total[3 * n:, LANES:]
        packed = (
            sorted_fields[:n] + sorted_fields[n:2 * n] * float(LANES) + sorted_fields[2 * n:] * float(rows_dev)
        ).astype(jnp.int32)
        for t in range(n):
            ids_out[t] = packed[t:t + 1]
        ids_in[me] = ids_out[me]

    pl.run_scoped(
        sort,
        (pltpu.ACC(0)((TILE, TILE), jnp.float32),) * (owned * n // TILE // 2),
        (pltpu.ACC(1)((TILE, TILE), jnp.float32),) * (owned * n // TILE // 2),
        pltpu.ACC(0)((6 * n, TILE), jnp.float32),
        pltpu.ACC(1)((6 * n, TILE), jnp.float32))

    mark("sends2")
    for d in neighbours:
        send_ids(d)
    for k in range(1, tiles):
        @pl.when(my_tile >= k)
        def _():
            for d in plane_of(my_tile - k):
                send_ids(d)

    def reach_up(k):
        @pl.when(my_tile + k < tiles)
        def _():
            pl.semaphore_wait(in_sem.at[my_tile + k], 1)
            for d in same_core_of(my_tile + k):
                send_queries(d, q_recv.at[my_tile])
            for d in plane_of(my_tile + k):
                send_ids(d)

    def hand_over(p):
        blocks_of = q_in.at[pl.ds(core * chips + planes[p] * dpc, dpc)]
        bulk_wait(blocks_of, q_recv.at[planes[p]])
        pltpu.make_async_remote_copy(
            src_ref=blocks_of, dst_ref=blocks_of, send_sem=hand_send, recv_sem=hand_recv.at[planes[p]],
            device_id=where_is(me + 1 - 2 * core), device_id_type=MESH).start()

    left = lax.broadcasted_iota(jnp.int32, (owned, LANES), 1) < half

    def unpack(chip):
        f0 = q_in[chip].astype(jnp.float32)
        f1 = q_in[chips + chip].astype(jnp.float32)
        both = jnp.concatenate(
            [jnp.where(left, f0, pltpu.roll(f1, half, 1)), jnp.where(left, pltpu.roll(f0, half, 1), f1)], axis=0)
        q_full[pl.ds(pl.multiple_of(chip * 2 * owned, 2 * owned), 2 * owned), :] = both.astype(jnp.bfloat16)

    order = [(0, None), (0, None), (1, 0), (1, 1), (2, 0), (3, 0), (3, 1), (2, 1)]

    def arrive(b):
        p, side = order[b]
        if b == 0:
            bulk_wait(q_in.at[pl.ds(0, dph - 1)], q_recv.at[tiles])
            first, many = my_tile * dpc + my_half * (dpc // 2), dpc // 2
        elif b == 1:
            bulk_wait(q_in.at[pl.ds(0, dph)], q_recv.at[tiles + 1])
            first, many = my_tile * dpc + (1 - my_half) * (dpc // 2), dpc // 2
        elif side == 0:
            bulk_wait(q_in.at[pl.ds(0, dpc)], hand_recv.at[planes[p]])
            first, many = planes[p] * dpc, dpc
        else:
            many = 0
        for g in range(many):
            unpack(first + g)

    def block_of(b):
        p, side = order[b]
        if b == 0:
            return my_tile * 2 + my_half
        if b == 1:
            return my_tile * 2 + 1 - my_half
        return planes[p] * 2 + side

    def stage_ids(u):
        take = dpt - 1 if u == 0 else dpt
        bulk_wait(ids_in.at[pl.ds(0, take)], ids_recv.at[askers[u]])
        ids_at[pl.ds(u * dpt, dpt)] = jnp.bitwise_and(
            ids_in[pl.ds(pl.multiple_of(askers[u] * dpt, dpt), dpt)], jnp.int32(rows_dev - 1))
        to_smem(u).start()

    def to_smem(u):
        at = pl.ds(u * dpt, dpt)
        return pltpu.make_async_copy(ids_at.at[at], ids_sm.at[at], sm_sem.at[u])

    def send_vals(u):
        if u == 0:
            vals_in[me] = vals_out[my_j]
        for j in range(1 if u == 0 else 0, dpt):
            at = (my_j + j) % dpt
            pltpu.make_async_remote_copy(
                src_ref=vals_out.at[u * dpt + at], dst_ref=vals_in.at[me], send_sem=vals_send, recv_sem=vals_recv,
                device_id=where_is(askers[u] * dpt + at), device_id_type=MESH).start()

    who_q = lax.broadcasted_iota(jnp.int32, (owned, LANES), 0)
    in_use = lax.broadcasted_iota(jnp.int32, (owned, LANES), 1) < capacity
    zeros = jnp.zeros((LANES, LANES), jnp.bfloat16)

    def diagonal(a, b):
        z = zeros[:a.shape[0]]
        return jnp.concatenate([jnp.concatenate([a, z], axis=1), jnp.concatenate([z, b], axis=1)], axis=0)

    def stream(*accs):
        ranges = (accs[:RANGES], accs[RANGES:2 * RANGES])
        extra = accs[2 * RANGES:]
        turn = [0, 0]
        staged = [[], []]
        pending = []
        sums = {}
        count = [0, 0]

        def push(m, value):
            r = turn[m]
            turn[m] = 1 - r
            pltpu.matmul_push_rhs(value, staging_register=r, mxu_index=m, transpose=True)
            staged[m].append(r)
            assert len(staged[m]) <= 2

        def weights(b):
            at = block_of(b)
            q = q_full[pl.ds(pl.multiple_of(at * LANES, LANES), LANES), :]
            return diagonal(q, q)

        def pop():
            kind, m, ref, data = pending.pop(0)
            got = pltpu.matmul_pop(ref)
            if kind == "sweep":
                over = jnp.maximum(got - data[1], 0.0).reshape(ROWS // 16, 2, 8, 2 * LANES)
                part = jnp.sum(over, axis=0)
                sums[data[0]] = sums[data[0]] + part if data[0] in sums else part
            else:
                u, a = data
                for e in range(2):
                    j = 2 * a + e
                    who = lax.shift_right_arithmetic(
                        ids_in[askers[u] * dpt + j], jnp.int32(id_bits))
                    picked = jnp.where((who == who_q) & in_use, got[:, e * LANES:(e + 1) * LANES], 0.0)
                    vals_out[u * dpt + j] = jnp.sum(picked, axis=0, keepdims=True)

        def drain(depth):
            while len(pending) > depth:
                pop()

        def finish(b):
            acc = sums.pop(b)
            acc = acc[0] + acc[1]
            acc = acc[:, :LANES] + acc[:, LANES:]
            at = block_of(b)
            mass_rows[b] = jnp.sum(acc, axis=0, keepdims=True)
            if b == 0:
                mass_in[me] = mass_rows[b]
                dests = own_half
            else:
                dests = [at * dph + (my_h + i) % dph for i in range(dph)]
            for d in dests:
                pltpu.make_async_remote_copy(
                    src_ref=mass_rows.at[b], dst_ref=mass_in.at[me],
                    send_sem=mass_send, recv_sem=mass_recv,
                    device_id=where_is(d), device_id_type=MESH).start()

        def gather(u, k):
            j, r = k // capacity, k % capacity
            rows_v[u * dpt + j, pl.ds(r, 1), :] = corpus_f[pl.ds(ids_sm[u * dpt + j, 0, r], 1), :]

        def widen(k):
            size = rows_dev // (2 * PIECES)
            at = pl.ds(k * size, size)
            corpus_f[at, :] = corpus_v[at, :].astype(jnp.float32)

        def ask(u, a):
            m = a % 2
            at = u * dpt + 2 * a
            push(m, diagonal(rows_v[at].astype(jnp.bfloat16), rows_v[at + 1].astype(jnp.bfloat16)))
            push(m, current[0])

        def reply(u, a):
            m = a % 2
            first = askers[u] * dpt + 2 * a
            q = q_full[pl.ds(pl.multiple_of(first * owned, 2 * owned), 2 * owned), :]
            pltpu.matmul_acc_lhs(
                extra[m], jnp.concatenate([q[:owned], q[owned:]], axis=1), load_staged_rhs=staged[m].pop(0))
            pending.append(("pair", m, extra[m], (u, a)))

        current = [None]
        acts = dict(reach=reach_up, hand=hand_over, ids=stage_ids, sm=lambda u: to_smem(u).wait(), vals=send_vals)
        gathers, asks, replies, reload = {}, {}, {}, set()
        per_step = 2 * dpt * capacity // (2 * PIECES)
        for u, s0 in enumerate(UNITS):
            for i in range(PIECES):
                gathers[s0 + i] = (u, i * per_step, (i + 1) * per_step)
            for a in range(dpt // 2):
                s1 = s0 + (a + 1) * PIECES * 2 // dpt + 1
                asks[s1] = (u, a)
                s1 += 6
                s1 += (s1 + a) % 2
                replies[s1] = (u, a)
                reload.add(s1)

        for b in range(2 * tiles):
            cut = None
            for piece in range(PIECES):
                step = b * PIECES + piece
                for name, arg in PLAN.get(step, ()):
                    mark(f"{name}{arg}")
                    acts[name](arg)
                    mark(f"go{step}")
                if piece == 0:
                    mark(f"arrive{b}")
                    arrive(b)
                    if b == 0:
                        load.wait()
                    mark(f"block{b}")
                    current[0] = weights(b)
                    for m in range(2):
                        push(m, current[0])
                    cut = thr_ref[:, pl.ds(pl.multiple_of(block_of(b) * LANES, LANES), LANES)].astype(jnp.float32) * 0.01
                    cut = jnp.concatenate([cut, cut], axis=1)
                m = piece % 2
                if step in replies:
                    reply(*replies[step])
                at = pl.ds(piece * ROWS, ROWS)
                lhs = jnp.concatenate(
                    [corpus_v[at, :], corpus_v[pl.ds(rows_dev // 2 + piece * ROWS, ROWS), :]], axis=1)
                ref = ranges[m][count[m] % RANGES]
                count[m] += 1
                pltpu.matmul_acc_lhs(ref, lhs, load_staged_rhs=staged[m].pop(0) if piece < 2 or step in reload else None)
                pending.append(("sweep", m, ref, (b, cut)))
                if step in asks:
                    ask(*asks[step])
                if step in gathers:
                    u, k0, k1 = gathers[step]
                    for k in range(k0, k1):
                        gather(u, k)
                if step < 2 * PIECES:
                    widen(step)
                drain(2 * LAG)
                if piece == 2 * LAG - 1 and b > 0:
                    finish(b - 1)
        drain(0)
        finish(2 * tiles - 1)

    pl.run_scoped(
        stream,
        *[pltpu.ACC(0)((ROWS, TILE), jnp.float32)] * RANGES,
        *[pltpu.ACC(1)((ROWS, TILE), jnp.float32)] * RANGES,
        pltpu.ACC(0)((owned, TILE), jnp.float32),
        pltpu.ACC(1)((owned, TILE), jnp.float32))

    mark("valswait")
    bulk_wait(vals_in.at[pl.ds(0, n - 1)], vals_recv)
    mark("spread")
    values = jnp.concatenate([vals_in[t] for t in range(n)], axis=0)
    top = values.astype(jnp.bfloat16)
    rest = values - top.astype(jnp.float32)
    mid = rest.astype(jnp.bfloat16)
    last = (rest - mid.astype(jnp.float32)).astype(jnp.bfloat16)
    upper_part = jnp.concatenate([top, mid], axis=1)
    lower_part = jnp.concatenate([last, jnp.zeros_like(last)], axis=1)
    cand = cand_pad[...]
    target = lax.shift_right_arithmetic(cand, jnp.int32(id_bits))
    dest = lax.broadcasted_iota(jnp.int32, (n, LANES), 0)

    def spread(*refs):
        for i in range(owned // 2):
            place = places[:, 2 * i * LANES:2 * (i + 1) * LANES]
            pltpu.matmul_push_rhs(
                jnp.concatenate([place, place], axis=0), staging_register=i // 2 % 2, mxu_index=i % 2)
            pltpu.matmul_acc_lhs(refs[i % 2][i // 2], upper_part, load_staged_rhs=i // 2 % 2)
            pltpu.matmul_acc_lhs(refs[i % 2][i // 2], lower_part)
        for i in range(owned // 2):
            both = pltpu.matmul_pop(refs[i % 2][i // 2])
            for e in range(2):
                q = 2 * i + e
                ans_out[q:q + 1, :] = jnp.sum(
                    jnp.where(target[q:q + 1] == dest, both[:, e * LANES:(e + 1) * LANES], 0.0),
                    axis=0, keepdims=True)[:, :per_query]

    pl.run_scoped(
        spread,
        (pltpu.ACC(0)((n, TILE), jnp.float32),) * (owned // 4),
        (pltpu.ACC(1)((n, TILE), jnp.float32),) * (owned // 4))

    store_ans = pltpu.make_async_copy(ans_out, ans_hbm, out_sem.at[0])
    store_ans.start()
    mark("masswait")
    bulk_wait(mass_in.at[pl.ds(0, n - 1)], mass_recv)
    mark("masssum")
    mass = mass_in[0]
    for t in range(1, n):
        mass = mass + mass_in[t]
    mass = mass * (8.0 / npass_all)
    per_row = LANES // owned
    result = mass
    for u in range(1, per_row):
        result = jnp.where(me % per_row == u, pltpu.roll(mass, LANES - u * owned, 1), result)
    mass_out[...] = result[:, :owned]
    store_mass = pltpu.make_async_copy(mass_out, mass_hbm, out_sem.at[1])
    store_mass.start()

    mark("sendwaits")
    bulk_wait(q_in.at[pl.ds(0, dpt - 1 + (tiles - 1) * dpc)], q_send)
    bulk_wait(q_in.at[pl.ds(0, (tiles - 1) * dpc)], hand_send)
    bulk_wait(ids_in.at[pl.ds(0, n - 1)], ids_send)
    bulk_wait(vals_in.at[pl.ds(0, n - 1)], vals_send)
    bulk_wait(mass_in.at[pl.ds(0, n - 1)], mass_send)
    store_ans.wait()
    store_mass.wait()
    mark(None)


def fused_body(n, nf, queries, corpus, candidates, threshold):
    rows_dev, width = corpus.shape
    owned, per_query = candidates.shape
    nq = n * owned
    tiles = nq // TILE
    capacity = (owned * per_query + n - 1) // n
    mass, answers = pl.pallas_call(
        functools.partial(kernel, n, nf, rows_dev * n, capacity),
        out_shape=(
            jax.ShapeDtypeStruct((1, owned), jnp.float32),
            jax.ShapeDtypeStruct((owned, per_query), jnp.float32),
        ),
        in_specs=[pl.BlockSpec(memory_space=pl.ANY)] * 4,
        out_specs=[pl.BlockSpec(memory_space=pl.ANY)] * 2,
        scratch_shapes=[
            pltpu.VMEM((1, owned), jnp.float32),
            pltpu.VMEM((owned, per_query), jnp.float32),
            pltpu.VMEM(queries.shape, jnp.bfloat16),
            pltpu.VMEM((1, nq), jnp.int32),
            pltpu.VMEM((owned, per_query), jnp.int32),
            pltpu.VMEM((rows_dev, width), jnp.bfloat16),
            pltpu.VMEM((rows_dev, width), jnp.float32),
            pltpu.VMEM((owned, LANES), jnp.bfloat16),
            pltpu.VMEM((n, owned, LANES), jnp.bfloat16),
            pltpu.VMEM((nq, LANES), jnp.bfloat16),
            pltpu.VMEM((owned, LANES), jnp.int32),
            pltpu.VMEM((LANES, owned * LANES), jnp.bfloat16),
            pltpu.VMEM((n, 1, LANES), jnp.int32),
            pltpu.VMEM((n, 1, LANES), jnp.int32),
            pltpu.VMEM((n, 1, LANES), jnp.int32),
            pltpu.SMEM((n, 1, LANES), jnp.int32),
            pltpu.VMEM((n, LANES, LANES), jnp.float32),
            pltpu.VMEM((n, 1, LANES), jnp.float32),
            pltpu.VMEM((n, 1, LANES), jnp.float32),
            pltpu.VMEM((nq // LANES, 1, LANES), jnp.float32),
            pltpu.VMEM((n, 1, LANES), jnp.float32),
            pltpu.SemaphoreType.DMA((3,)),
            pltpu.SemaphoreType.DMA,
            pltpu.SemaphoreType.DMA((2,)),
            pltpu.SemaphoreType.DMA((tiles,)),
            pltpu.SemaphoreType.REGULAR((tiles,)),
            pltpu.SemaphoreType.DMA,
            pltpu.SemaphoreType.DMA((tiles + 2,)),
            pltpu.SemaphoreType.DMA,
            pltpu.SemaphoreType.DMA((tiles,)),
            pltpu.SemaphoreType.DMA,
            pltpu.SemaphoreType.DMA((tiles,)),
            pltpu.SemaphoreType.DMA,
            pltpu.SemaphoreType.DMA,
            pltpu.SemaphoreType.DMA,
            pltpu.SemaphoreType.DMA,
        ],
        compiler_params=pltpu.CompilerParams(
            collective_id=0, has_side_effects=True),
    )(queries, threshold.reshape(1, nq), candidates, corpus)
    return mass.reshape(owned), answers


def plain_body(queries, corpus, candidates, threshold):
    rows_dev = corpus.shape[0]
    width = corpus.shape[1]
    shards = lax.axis_size("rows") * lax.axis_size("feat")
    owned_queries = candidates.shape[0]
    per_query = candidates.shape[1]
    npass_all = rows_dev * shards
    cutoff = threshold.astype(jnp.float32) * 0.01
    owner = lax.axis_index(("rows", "feat"))
    full_rows = lax.all_gather(queries, "feat", axis=1, tiled=True)
    whole = lax.all_gather(full_rows, "rows", axis=0, tiled=True)
    query_count = whole.shape[0]
    block = 2048
    corpus_blocks = corpus.reshape(rows_dev // block, block, width)

    def visit(total, block_rows):
        scores = lax.dot_general(
            whole, block_rows, (((1,), (1,)), ((), ())), preferred_element_type=jnp.float32
        )
        return (total + jnp.sum(jnp.maximum(scores - cutoff[:, None], 0.0), axis=1), None)

    total, _ = lax.scan(visit, jnp.zeros((query_count,), jnp.float32), corpus_blocks)
    flat_ids = candidates.reshape(-1)
    total_ids = flat_ids.shape[0]
    capacity = (total_ids + shards - 1) // shards
    target = flat_ids // rows_dev
    onehot = (target[:, None] == jnp.arange(shards, dtype=jnp.int32)[None, :]).astype(jnp.int32)
    before = jnp.cumsum(onehot, axis=0) - onehot
    rank = jnp.sum(before * onehot, axis=1)
    query_ids = owner * owned_queries + jnp.arange(total_ids, dtype=jnp.int32) // per_query
    fields = jnp.stack([flat_ids - target * rows_dev, query_ids], axis=1)
    send_both = jnp.zeros((shards, capacity, 2), jnp.int32).at[target, rank].set(fields)
    n_rows = lax.axis_size("rows")
    n_feat = lax.axis_size("feat")
    received = lax.all_to_all(
        lax.all_to_all(
            send_both.reshape(n_rows, n_feat, capacity * 2),
            "rows",
            split_axis=0,
            concat_axis=0,
            tiled=True,
        ),
        "feat",
        split_axis=1,
        concat_axis=1,
        tiled=True,
    )
    received = received.reshape(shards * capacity, 2)
    picked = corpus[received[:, 0]]
    asked = whole[received[:, 1]]
    values = jnp.einsum("kd,kd->k", picked, asked, preferred_element_type=jnp.float32).reshape(
        n_rows, n_feat, capacity
    )
    partials = total.reshape(n_rows, n_feat, owned_queries)
    answers, mass_parts = (
        lax.all_to_all(
            lax.all_to_all(values, "rows", split_axis=0, concat_axis=0, tiled=True),
            "feat",
            split_axis=1,
            concat_axis=1,
            tiled=True,
        ),
        lax.all_to_all(
            lax.all_to_all(partials, "rows", split_axis=0, concat_axis=0, tiled=True),
            "feat",
            split_axis=1,
            concat_axis=1,
            tiled=True,
        ),
    )
    exceed = jnp.sum(mass_parts, axis=(0, 1)) * (8.0 / npass_all)
    candidate_scores = answers.reshape(shards, capacity)[target, rank].reshape(
        owned_queries, per_query
    )
    return (exceed, candidate_scores)


def body(queries, corpus, candidates, threshold):
    nf = lax.axis_size("feat")
    n = lax.axis_size("rows") * nf
    rows_dev, width = corpus.shape
    owned, per_query = candidates.shape
    capacity = (owned * per_query + n - 1) // n
    fits = (
        nf == 2
        and width == LANES
        and queries.shape == (2 * owned, LANES // 2)
        and owned % 32 == 0
        and LANES % owned == 0
        and per_query <= LANES
        and capacity <= LANES
        and n % 8 == 0
        and (n * owned) % TILE == 0
        and n * owned == 4 * TILE
        and rows_dev == 2 * ROWS * PIECES
        and rows_dev & (rows_dev - 1) == 0
    )
    if fits:
        return fused_body(n, nf, queries, corpus, candidates, threshold)
    return plain_body(queries, corpus, candidates, threshold)


def solution(mesh):
    return jax.shard_map(
        body,
        mesh=mesh,
        in_specs=(P("rows", "feat"), P(("rows", "feat"), None), P(("rows", "feat"), None), P()),
        out_specs=(P(("rows", "feat")), P(("rows", "feat"), None)),
        check_vma=False,
    )
```

time: 31.3 us -> 28.6 us (0.914)
  Pallas kernels: 27.9 us -> 25.2 us
    pallas_call x1, Pallas kernels: 27.9 us -> 25.2 us  [fused_body(): pl.pallas_call(functools.partial(kernel, n, nf, rows_dev * n, capacity),...]
    unnamed x1 -> x2, local copies, waits for them, and re-layouts: 1.32 us -> 2.46 us
    squeeze x1 -> x0, local copies, waits for them, and re-layouts: 1.14 us -> none  [fused_body(): return (mass[0, :owned], answers[:, :per_query])]
where the time goes in v1:
time: 28.6 us; the launch traced here: 28.3 us
  Pallas kernels  25.2 us (88%)
  local copies, waits for them, and re-layouts  2.46 us (9%)
  between operations  0.64 us (2%)
    pallas_call x1, Pallas kernels, fused_body(): pl.pallas_call(functools.partial(kernel, n, nf, rows_dev * n, capacity),...  25.2 us
    unnamed x2, local copies, waits for them, and re-layouts  2.46 us

profile of v1, /device:TPU:0, one launch (start us, length us, event | category | flops | bytes accessed | tf_op | source)
XLA Modules:
  0.0 28.3 jit_solution(9527258676757533607)
XLA Ops:
  0.6 25.2 %shard_map.59 = (f32[1,32]{1,0:T(1,128)}, f32[32,100]{1,0:T(8,128)}) custom-call(bf16[64,64]{1,0:T(8,128)(2,1)} %q_hbm.1, s32[1,1024]{1,0:T(1,128)} %bitcast.2, s32[32,100]{1,0:T(8,128)} %cand_hbm.1, bf16[16384,128]{1,0:T(8,128)(2,1)} %corpus_ref.1), custom_call_target="tpu_custom_call" | custom-call | tf_op jit(solution)/shard_map/pallas_call | solution.py:509
  25.8 1.1 %copy.8 = f32[32]{0:T(128)} copy(f32[32]{0:T(128)} %bitcast.3) | data formatting | bytes 256
  26.9 1.3 %copy.9 = f32[32,100]{1,0:T(8,128)} copy(f32[32,100]{1,0:T(8,128)} %get-tuple-element.9) | data formatting | bytes 25600

commit v2 on v1

--- a/solution.py
+++ b/solution.py
@@ -13,15 +13,30 @@
 PIECES = 32
 RANGES = 3
 LAG = 2
-UNITS = (88, 120, 152, 184)
+AHEAD = 5
+UNITS = {
+    0: (74, 32, (96, 112)), 1: (108, 16, (128, 144)), 2: (154, 32, (176, 192)), 3: (186, 32, (208, 224)),
+}
 PLAN = {
-    0: (("reach", 1),), 40: (("reach", 2),), 48: (("hand", 1),), 72: (("reach", 3),), 96: (("hand", 2),),
-    124: (("hand", 3),),
-    70: (("ids", 0),), 84: (("sm", 0),), 104: (("ids", 1),), 118: (("sm", 1),),
-    136: (("ids", 2),), 150: (("sm", 2),), 168: (("ids", 3),), 182: (("sm", 3),),
-    134: (("vals", 0),), 166: (("vals", 1),), 198: (("vals", 2),), 230: (("vals", 3),),
+    20: (("arrive", 1),),
+    38: (("mass", 0), ("reach", 2), ("hand", 1)),
+    54: (("reach", 3), ("ids", 0)),
+    58: (("arrive", 2),),
+    70: (("mass", 1), ("sm", 0)),
+    100: (("ids", 1), ("hand", 2)),
+    106: (("mass", 2), ("sm", 1)),
+    118: (("vals", 0),),
+    122: (("arrive", 4),),
+    134: (("mass", 3), ("ids", 2)),
+    150: (("vals", 1), ("hand", 3), ("sm", 2)),
+    166: (("mass", 4), ("ids", 3)),
+    172: (("arrive", 6),),
+    182: (("sm", 3),),
+    198: (("mass", 5), ("vals", 2)),
+    230: (("mass", 6), ("vals", 3)),
 }
-MESH = pl.DeviceIdType.MESH
+FENCES = frozenset(range(0, 224, 8))
+LOGICAL = pl.DeviceIdType.LOGICAL
 
 
 def mark(name):
@@ -35,11 +50,10 @@
 def kernel(
     n, nf, npass_all, capacity,
     q_hbm, thr_hbm, cand_hbm, corpus_ref,
-    mass_hbm, ans_hbm,
     mass_out, ans_out,
     q_ref, thr_ref, cand_ref, corpus_v, corpus_f, q_pack, q_in, q_full, cand_pad, places,
     ids_out, ids_in, ids_at, ids_sm, rows_v, vals_out, vals_in, mass_rows, mass_in,
-    small_sem, load_sem, out_sem, sm_sem, in_sem, q_send, q_recv, hand_send, hand_recv,
+    small_sem, load_sem, sm_sem, in_sem, fence_sem, q_send, q_recv, hand_send, hand_recv,
     ids_send, ids_recv, vals_send, vals_recv, mass_send, mass_recv,
 ):
     rows_dev, width = corpus_v.shape
@@ -65,8 +79,8 @@
             out = out + (values[k] - values[k - 1]) * ((my_tile + tiles - 1 - k) // (tiles - 1))
         return out
 
-    planes = [my_tile, table((1, 0, 1, 2)), table((2, 2, 0, 1)), table((3, 3, 3, 0))]
-    askers = [my_tile, table((1, 0, 1, 2)), table((2, 2, 0, 0)), table((3, 3, 3, 1))]
+    planes = [my_tile, table((1, 0, 1, 2)), table((2, 2, 0, 0)), table((3, 3, 3, 1))]
+    askers = planes[1:] + planes[:1]
 
     load = pltpu.make_async_copy(corpus_ref, corpus_v, load_sem)
     small = [
@@ -76,11 +90,9 @@
         copy.start()
     load.start()
 
-    def where_is(d):
-        return (d // nf, d % nf)
-
-    own_half = [my_tile * dpt + my_half * dph + (my_h + i) % dph for i in range(1, dph)]
-    other_half = [my_tile * dpt + (1 - my_half) * dph + (my_h + i) % dph for i in range(dph)]
+    around = [(my_h + i) % dph for i in range(dph)]
+    own_half = [my_tile * dpt + my_half * dph + j for j in around[1:]]
+    other_half = [my_tile * dpt + (1 - my_half) * dph + j for j in around]
     neighbours = own_half + other_half
 
     def plane_of(t):
@@ -92,7 +104,7 @@
     barrier = pltpu.get_barrier_semaphore()
 
     def signal(sem, d):
-        pl.semaphore_signal(sem, inc=1, device_id=where_is(d), device_id_type=MESH)
+        pl.semaphore_signal(sem, inc=1, device_id=(d), device_id_type=LOGICAL)
 
     mark("start")
     for d in neighbours:
@@ -120,12 +132,12 @@
     def send_queries(d, sem):
         pltpu.make_async_remote_copy(
             src_ref=q_pack, dst_ref=q_in.at[my_place], send_sem=q_send, recv_sem=sem,
-            device_id=where_is(d), device_id_type=MESH).start()
+            device_id=(d), device_id_type=LOGICAL).start()
 
     def send_ids(d):
         pltpu.make_async_remote_copy(
             src_ref=ids_out.at[d], dst_ref=ids_in.at[me], send_sem=ids_send, recv_sem=ids_recv.at[my_tile],
-            device_id=where_is(d), device_id_type=MESH).start()
+            device_id=(d), device_id_type=LOGICAL).start()
 
     for d in own_half:
         send_queries(d, q_recv.at[tiles])
@@ -227,7 +239,7 @@
         bulk_wait(blocks_of, q_recv.at[planes[p]])
         pltpu.make_async_remote_copy(
             src_ref=blocks_of, dst_ref=blocks_of, send_sem=hand_send, recv_sem=hand_recv.at[planes[p]],
-            device_id=where_is(me + 1 - 2 * core), device_id_type=MESH).start()
+            device_id=(me + 1 - 2 * core), device_id_type=LOGICAL).start()
 
     left = lax.broadcasted_iota(jnp.int32, (owned, LANES), 1) < half
 
@@ -238,7 +250,7 @@
             [jnp.where(left, f0, pltpu.roll(f1, half, 1)), jnp.where(left, pltpu.roll(f0, half, 1), f1)], axis=0)
         q_full[pl.ds(pl.multiple_of(chip * 2 * owned, 2 * owned), 2 * owned), :] = both.astype(jnp.bfloat16)
 
-    order = [(0, None), (0, None), (1, 0), (1, 1), (2, 0), (3, 0), (3, 1), (2, 1)]
+    order = [(b // 2, b % 2) for b in range(2 * tiles)]
 
     def arrive(b):
         p, side = order[b]
@@ -265,7 +277,7 @@
         return planes[p] * 2 + side
 
     def stage_ids(u):
-        take = dpt - 1 if u == 0 else dpt
+        take = dpt - 1 if u == tiles - 1 else dpt
         bulk_wait(ids_in.at[pl.ds(0, take)], ids_recv.at[askers[u]])
         ids_at[pl.ds(u * dpt, dpt)] = jnp.bitwise_and(
             ids_in[pl.ds(pl.multiple_of(askers[u] * dpt, dpt), dpt)], jnp.int32(rows_dev - 1))
@@ -276,13 +288,13 @@
         return pltpu.make_async_copy(ids_at.at[at], ids_sm.at[at], sm_sem.at[u])
 
     def send_vals(u):
-        if u == 0:
-            vals_in[me] = vals_out[my_j]
-        for j in range(1 if u == 0 else 0, dpt):
+        if u == tiles - 1:
+            vals_in[me] = vals_out[u * dpt + my_j]
+        for j in range(1 if u == tiles - 1 else 0, dpt):
             at = (my_j + j) % dpt
             pltpu.make_async_remote_copy(
                 src_ref=vals_out.at[u * dpt + at], dst_ref=vals_in.at[me], send_sem=vals_send, recv_sem=vals_recv,
-                device_id=where_is(askers[u] * dpt + at), device_id_type=MESH).start()
+                device_id=(askers[u] * dpt + at), device_id_type=LOGICAL).start()
 
     who_q = lax.broadcasted_iota(jnp.int32, (owned, LANES), 0)
     in_use = lax.broadcasted_iota(jnp.int32, (owned, LANES), 1) < capacity
@@ -330,8 +342,11 @@
                     vals_out[u * dpt + j] = jnp.sum(picked, axis=0, keepdims=True)
 
         def drain(depth):
-            while len(pending) > depth:
+            while sum(kind == "sweep" for kind, *_ in pending) > depth:
                 pop()
+            if depth == 0:
+                while pending:
+                    pop()
 
         def finish(b):
             acc = sums.pop(b)
@@ -343,12 +358,12 @@
                 mass_in[me] = mass_rows[b]
                 dests = own_half
             else:
-                dests = [at * dph + (my_h + i) % dph for i in range(dph)]
+                dests = [at * dph + j for j in around]
             for d in dests:
                 pltpu.make_async_remote_copy(
                     src_ref=mass_rows.at[b], dst_ref=mass_in.at[me],
                     send_sem=mass_send, recv_sem=mass_recv,
-                    device_id=where_is(d), device_id_type=MESH).start()
+                    device_id=(d), device_id_type=LOGICAL).start()
 
         def gather(u, k):
             j, r = k // capacity, k % capacity
@@ -359,75 +374,63 @@
             at = pl.ds(k * size, size)
             corpus_f[at, :] = corpus_v[at, :].astype(jnp.float32)
 
-        def ask(u, a):
-            m = a % 2
-            at = u * dpt + 2 * a
-            push(m, diagonal(rows_v[at].astype(jnp.bfloat16), rows_v[at + 1].astype(jnp.bfloat16)))
-            push(m, current[0])
-
-        def reply(u, a):
-            m = a % 2
+        def stage(b, m, pair):
+            if pair is not None:
+                at = pair[0] * dpt + 2 * pair[1]
+                push(m, diagonal(rows_v[at].astype(jnp.bfloat16), rows_v[at + 1].astype(jnp.bfloat16)))
+            push(m, weights(b))
+
+        def reply(m, u, a):
             first = askers[u] * dpt + 2 * a
             q = q_full[pl.ds(pl.multiple_of(first * owned, 2 * owned), 2 * owned), :]
             pltpu.matmul_acc_lhs(
                 extra[m], jnp.concatenate([q[:owned], q[owned:]], axis=1), load_staged_rhs=staged[m].pop(0))
             pending.append(("pair", m, extra[m], (u, a)))
 
-        current = [None]
-        acts = dict(reach=reach_up, hand=hand_over, ids=stage_ids, sm=lambda u: to_smem(u).wait(), vals=send_vals)
-        gathers, asks, replies, reload = {}, {}, {}, set()
-        per_step = 2 * dpt * capacity // (2 * PIECES)
-        for u, s0 in enumerate(UNITS):
-            for i in range(PIECES):
-                gathers[s0 + i] = (u, i * per_step, (i + 1) * per_step)
-            for a in range(dpt // 2):
-                s1 = s0 + (a + 1) * PIECES * 2 // dpt + 1
-                asks[s1] = (u, a)
-                s1 += 6
-                s1 += (s1 + a) % 2
-                replies[s1] = (u, a)
-                reload.add(s1)
-
-        for b in range(2 * tiles):
-            cut = None
-            for piece in range(PIECES):
-                step = b * PIECES + piece
-                for name, arg in PLAN.get(step, ()):
-                    mark(f"{name}{arg}")
-                    acts[name](arg)
-                    mark(f"go{step}")
-                if piece == 0:
-                    mark(f"arrive{b}")
-                    arrive(b)
-                    if b == 0:
-                        load.wait()
-                    mark(f"block{b}")
-                    current[0] = weights(b)
-                    for m in range(2):
-                        push(m, current[0])
-                    cut = thr_ref[:, pl.ds(pl.multiple_of(block_of(b) * LANES, LANES), LANES)].astype(jnp.float32) * 0.01
-                    cut = jnp.concatenate([cut, cut], axis=1)
-                m = piece % 2
-                if step in replies:
-                    reply(*replies[step])
-                at = pl.ds(piece * ROWS, ROWS)
-                lhs = jnp.concatenate(
-                    [corpus_v[at, :], corpus_v[pl.ds(rows_dev // 2 + piece * ROWS, ROWS), :]], axis=1)
-                ref = ranges[m][count[m] % RANGES]
-                count[m] += 1
-                pltpu.matmul_acc_lhs(ref, lhs, load_staged_rhs=staged[m].pop(0) if piece < 2 or step in reload else None)
-                pending.append(("sweep", m, ref, (b, cut)))
-                if step in asks:
-                    ask(*asks[step])
-                if step in gathers:
-                    u, k0, k1 = gathers[step]
-                    for k in range(k0, k1):
+        acts = dict(
+            reach=reach_up, hand=hand_over, ids=stage_ids, sm=lambda u: to_smem(u).wait(), vals=send_vals,
+            mass=finish, arrive=arrive)
+        total = 2 * tiles * PIECES
+        answers = {h + m: (u, 2 * k + m) for u in UNITS for k, h in enumerate(UNITS[u][2]) for m in range(2)}
+        for step in range(total):
+            b, piece, m = step // PIECES, step % PIECES, step % 2
+            if step == 0:
+                mark("arrive0")
+                reach_up(1)
+                arrive(0)
+                load.wait()
+                for side in range(2):
+                    push(side, weights(0))
+            for name, arg in PLAN.get(step, ()):
+                mark(f"{name}{arg}")
+                acts[name](arg)
+            if step in PLAN or step == 0:
+                mark(f"go{step}")
+            if step in FENCES:
+                pl.semaphore_signal(fence_sem, inc=1)
+            if piece == 0:
+                at = pl.ds(pl.multiple_of(block_of(b) * LANES, LANES), LANES)
+                cut = thr_ref[:, at].astype(jnp.float32) * 0.01
+                cut = jnp.concatenate([cut, cut], axis=1)
+            if step in answers:
+                reply(m, *answers[step])
+            at = pl.ds(piece * ROWS, ROWS)
+            lhs = jnp.concatenate(
+                [corpus_v[at, :], corpus_v[pl.ds(rows_dev // 2 + piece * ROWS, ROWS), :]], axis=1)
+            ref = ranges[m][count[m] % RANGES]
+            count[m] += 1
+            pltpu.matmul_acc_lhs(ref, lhs, load_staged_rhs=staged[m].pop(0) if staged[m] and step % 16 < 2 else None)
+            pending.append(("sweep", m, ref, (b, cut)))
+            for u, (s0, length, _) in UNITS.items():
+                if s0 <= step < s0 + length:
+                    for k in range((step - s0) * dpt * capacity // length, (step - s0 + 1) * dpt * capacity // length):
                         gather(u, k)
-                if step < 2 * PIECES:
-                    widen(step)
-                drain(2 * LAG)
-                if piece == 2 * LAG - 1 and b > 0:
-                    finish(b - 1)
+            if step < 2 * PIECES:
+                widen(step)
+            ahead = step + AHEAD
+            if ahead % 16 < 2 and 16 <= ahead < total and (ahead % PIECES < 2 or ahead in answers):
+                stage(ahead // PIECES, ahead % 2, answers.get(ahead))
+            drain(2 * LAG)
         drain(0)
         finish(2 * tiles - 1)
 
@@ -472,8 +475,6 @@
         (pltpu.ACC(0)((n, TILE), jnp.float32),) * (owned // 4),
         (pltpu.ACC(1)((n, TILE), jnp.float32),) * (owned // 4))
 
-    store_ans = pltpu.make_async_copy(ans_out, ans_hbm, out_sem.at[0])
-    store_ans.start()
     mark("masswait")
     bulk_wait(mass_in.at[pl.ds(0, n - 1)], mass_recv)
     mark("masssum")
@@ -486,17 +487,14 @@
     for u in range(1, per_row):
         result = jnp.where(me % per_row == u, pltpu.roll(mass, LANES - u * owned, 1), result)
     mass_out[...] = result[:, :owned]
-    store_mass = pltpu.make_async_copy(mass_out, mass_hbm, out_sem.at[1])
-    store_mass.start()
 
     mark("sendwaits")
+    pl.semaphore_wait(fence_sem, len(FENCES))
     bulk_wait(q_in.at[pl.ds(0, dpt - 1 + (tiles - 1) * dpc)], q_send)
     bulk_wait(q_in.at[pl.ds(0, (tiles - 1) * dpc)], hand_send)
     bulk_wait(ids_in.at[pl.ds(0, n - 1)], ids_send)
     bulk_wait(vals_in.at[pl.ds(0, n - 1)], vals_send)
     bulk_wait(mass_in.at[pl.ds(0, n - 1)], mass_send)
-    store_ans.wait()
-    store_mass.wait()
     mark(None)
 
 
@@ -509,14 +507,12 @@
     mass, answers = pl.pallas_call(
         functools.partial(kernel, n, nf, rows_dev * n, capacity),
         out_shape=(
-            jax.ShapeDtypeStruct((1, owned), jnp.float32),
-            jax.ShapeDtypeStruct((owned, per_query), jnp.float32),
+            pltpu.VMEM((1, owned), jnp.float32),
+            pltpu.VMEM((owned, per_query), jnp.float32),
         ),
         in_specs=[pl.BlockSpec(memory_space=pl.ANY)] * 4,
-        out_specs=[pl.BlockSpec(memory_space=pl.ANY)] * 2,
+        out_specs=[pl.BlockSpec(memory_space=pltpu.VMEM)] * 2,
         scratch_shapes=[
-            pltpu.VMEM((1, owned), jnp.float32),
-            pltpu.VMEM((owned, per_query), jnp.float32),
             pltpu.VMEM(queries.shape, jnp.bfloat16),
             pltpu.VMEM((1, nq), jnp.int32),
             pltpu.VMEM((owned, per_query), jnp.int32),
@@ -538,9 +534,9 @@
             pltpu.VMEM((n, 1, LANES), jnp.float32),
             pltpu.SemaphoreType.DMA((3,)),
             pltpu.SemaphoreType.DMA,
-            pltpu.SemaphoreType.DMA((2,)),
             pltpu.SemaphoreType.DMA((tiles,)),
             pltpu.SemaphoreType.REGULAR((tiles,)),
+            pltpu.SemaphoreType.REGULAR,
             pltpu.SemaphoreType.DMA,
             pltpu.SemaphoreType.DMA((tiles + 2,)),
             pltpu.SemaphoreType.DMA,

time: 28.6 us -> 24.6 us (0.86)
  the two profiles are of different devices: /device:TPU:0 before, /device:TPU:12 now
where the time goes in v2:
time: 24.6 us; the launch traced here: 24.4 us
  Pallas kernels  22.6 us (92%)
  local copies, waits for them, and re-layouts  1.12 us (5%)
  between operations  0.64 us (3%)
    pallas_call x1, Pallas kernels, fused_body(): pl.pallas_call(functools.partial(kernel, n, nf, rows_dev * n, capacity),...  22.6 us
    unnamed x2, local copies, waits for them, and re-layouts  1.12 us

profile of v2, /device:TPU:12, one launch (start us, length us, event | category | flops | bytes accessed | tf_op | source)
XLA Modules:
  0.0 24.4 jit_solution(8456009330424747633)
XLA Ops:
  0.6 22.6 %shard_map.59 = (f32[1,32]{1,0:T(1,128)S(1)}, f32[32,100]{1,0:T(8,128)S(1)}) custom-call(bf16[64,64]{1,0:T(8,128)(2,1)} %q_hbm.1, s32[1,1024]{1,0:T(1,128)} %bitcast.3, s32[32,100]{1,0:T(8,128)} %cand_hbm.1, bf16[16384,128]{1,0:T(8,128)(2,1)} %corpus_ref.1), custom_call_target="tpu_custom_call" | custom-call | tf_op jit(solution)/shard_map/pallas_call | solution.py:507
  23.3 0.5 %copy.8 = f32[32]{0:T(128)} copy(f32[32]{0:T(128)S(1)} %bitcast.2) | data formatting | bytes 256
  23.8 0.6 %copy.9 = f32[32,100]{1,0:T(8,128)} copy(f32[32,100]{1,0:T(8,128)S(1)} %get-tuple-element.7) | data formatting | bytes 25600

commit v3 on v2

--- a/solution.py
+++ b/solution.py
@@ -11,19 +11,20 @@
 TILE = 256
 ROWS = 256
 PIECES = 32
+WIDEN = 512
 RANGES = 3
 LAG = 2
 AHEAD = 5
 UNITS = {
-    0: (74, 32, (96, 112)), 1: (108, 16, (128, 144)), 2: (154, 32, (176, 192)), 3: (186, 32, (208, 224)),
+    0: (74, 32, (96, 112)), 1: (106, 22, (128, 144)), 2: (154, 32, (176, 192)),
 }
 PLAN = {
     20: (("arrive", 1),),
-    38: (("mass", 0), ("reach", 2), ("hand", 1)),
-    54: (("reach", 3), ("ids", 0)),
+    38: (("mass", 0), ("reach", 2), ("hand", 1), ("reach", 3)),
+    54: (("ids", 0),),
     58: (("arrive", 2),),
     70: (("mass", 1), ("sm", 0)),
-    100: (("ids", 1), ("hand", 2)),
+    96: (("ids", 1), ("hand", 2)),
     106: (("mass", 2), ("sm", 1)),
     118: (("vals", 0),),
     122: (("arrive", 4),),
@@ -31,11 +32,10 @@
     150: (("vals", 1), ("hand", 3), ("sm", 2)),
     166: (("mass", 4), ("ids", 3)),
     172: (("arrive", 6),),
-    182: (("sm", 3),),
     198: (("mass", 5), ("vals", 2)),
-    230: (("mass", 6), ("vals", 3)),
+    230: (("mass", 6), ("sm", 3)),
 }
-FENCES = frozenset(range(0, 224, 8))
+FENCES = frozenset(range(0, 192, 8))
 LOGICAL = pl.DeviceIdType.LOGICAL
 
 
@@ -80,7 +80,7 @@
         return out
 
     planes = [my_tile, table((1, 0, 1, 2)), table((2, 2, 0, 0)), table((3, 3, 3, 1))]
-    askers = planes[1:] + planes[:1]
+    askers = [table(row) for row in ((0, 0, 1, 2), (1, 1, 0, 0), (2, 2, 2, 1), (3, 3, 3, 3))]
 
     load = pltpu.make_async_copy(corpus_ref, corpus_v, load_sem)
     small = [
@@ -229,10 +229,10 @@
         @pl.when(my_tile + k < tiles)
         def _():
             pl.semaphore_wait(in_sem.at[my_tile + k], 1)
+            for d in plane_of(my_tile + k):
+                send_ids(d)
             for d in same_core_of(my_tile + k):
                 send_queries(d, q_recv.at[my_tile])
-            for d in plane_of(my_tile + k):
-                send_ids(d)
 
     def hand_over(p):
         blocks_of = q_in.at[pl.ds(core * chips + planes[p] * dpc, dpc)]
@@ -277,8 +277,13 @@
         return planes[p] * 2 + side
 
     def stage_ids(u):
-        take = dpt - 1 if u == tiles - 1 else dpt
-        bulk_wait(ids_in.at[pl.ds(0, take)], ids_recv.at[askers[u]])
+        @pl.when(my_tile == u)
+        def _():
+            bulk_wait(ids_in.at[pl.ds(0, dpt - 1)], ids_recv.at[askers[u]])
+
+        @pl.when(my_tile != u)
+        def _():
+            bulk_wait(ids_in.at[pl.ds(0, dpt)], ids_recv.at[askers[u]])
         ids_at[pl.ds(u * dpt, dpt)] = jnp.bitwise_and(
             ids_in[pl.ds(pl.multiple_of(askers[u] * dpt, dpt), dpt)], jnp.int32(rows_dev - 1))
         to_smem(u).start()
@@ -288,13 +293,21 @@
         return pltpu.make_async_copy(ids_at.at[at], ids_sm.at[at], sm_sem.at[u])
 
     def send_vals(u):
-        if u == tiles - 1:
-            vals_in[me] = vals_out[u * dpt + my_j]
-        for j in range(1 if u == tiles - 1 else 0, dpt):
-            at = (my_j + j) % dpt
+        def send(at):
             pltpu.make_async_remote_copy(
                 src_ref=vals_out.at[u * dpt + at], dst_ref=vals_in.at[me], send_sem=vals_send, recv_sem=vals_recv,
                 device_id=(askers[u] * dpt + at), device_id_type=LOGICAL).start()
+
+        for j in range(1, dpt):
+            send((my_j + j) % dpt)
+
+        @pl.when(my_tile != u)
+        def _():
+            send(my_j)
+
+        @pl.when(my_tile == u)
+        def _():
+            vals_in[me] = vals_out[u * dpt + my_j]
 
     who_q = lax.broadcasted_iota(jnp.int32, (owned, LANES), 0)
     in_use = lax.broadcasted_iota(jnp.int32, (owned, LANES), 1) < capacity
@@ -369,23 +382,19 @@
             j, r = k // capacity, k % capacity
             rows_v[u * dpt + j, pl.ds(r, 1), :] = corpus_f[pl.ds(ids_sm[u * dpt + j, 0, r], 1), :]
 
-        def widen(k):
-            size = rows_dev // (2 * PIECES)
-            at = pl.ds(k * size, size)
-            corpus_f[at, :] = corpus_v[at, :].astype(jnp.float32)
-
         def stage(b, m, pair):
             if pair is not None:
                 at = pair[0] * dpt + 2 * pair[1]
                 push(m, diagonal(rows_v[at].astype(jnp.bfloat16), rows_v[at + 1].astype(jnp.bfloat16)))
             push(m, weights(b))
 
-        def reply(m, u, a):
+        def reply(m, u, a, spare=0):
+            ref = extra[m + 2 * spare]
             first = askers[u] * dpt + 2 * a
             q = q_full[pl.ds(pl.multiple_of(first * owned, 2 * owned), 2 * owned), :]
             pltpu.matmul_acc_lhs(
-                extra[m], jnp.concatenate([q[:owned], q[owned:]], axis=1), load_staged_rhs=staged[m].pop(0))
-            pending.append(("pair", m, extra[m], (u, a)))
+                ref, jnp.concatenate([q[:owned], q[owned:]], axis=1), load_staged_rhs=staged[m].pop(0))
+            pending.append(("pair", m, ref, (u, a)))
 
         acts = dict(
             reach=reach_up, hand=hand_over, ids=stage_ids, sm=lambda u: to_smem(u).wait(), vals=send_vals,
@@ -396,9 +405,7 @@
             b, piece, m = step // PIECES, step % PIECES, step % 2
             if step == 0:
                 mark("arrive0")
-                reach_up(1)
                 arrive(0)
-                load.wait()
                 for side in range(2):
                     push(side, weights(0))
             for name, arg in PLAN.get(step, ()):
@@ -425,8 +432,6 @@
                 if s0 <= step < s0 + length:
                     for k in range((step - s0) * dpt * capacity // length, (step - s0 + 1) * dpt * capacity // length):
                         gather(u, k)
-            if step < 2 * PIECES:
-                widen(step)
             ahead = step + AHEAD
             if ahead % 16 < 2 and 16 <= ahead < total and (ahead % PIECES < 2 or ahead in answers):
                 stage(ahead // PIECES, ahead % 2, answers.get(ahead))
@@ -434,12 +439,33 @@
         drain(0)
         finish(2 * tiles - 1)
 
+        mark("last")
+        u = tiles - 1
+        for k in range(dpt * capacity):
+            gather(u, k)
+        for a in range(dpt // 2):
+            at = u * dpt + 2 * a
+            push(a % 2, diagonal(rows_v[at].astype(jnp.bfloat16), rows_v[at + 1].astype(jnp.bfloat16)))
+            reply(a % 2, u, a, a // 2)
+        drain(0)
+        send_vals(u)
+
+    mark("reach1")
+    reach_up(1)
+    load.wait()
+    mark("widen")
+
+    def widen(b, carry):
+        at = pl.ds(pl.multiple_of(b * WIDEN, WIDEN), WIDEN)
+        corpus_f[at, :] = corpus_v[at, :].astype(jnp.float32)
+        return carry
+    lax.fori_loop(0, rows_dev // WIDEN, widen, 0)
+
     pl.run_scoped(
         stream,
         *[pltpu.ACC(0)((ROWS, TILE), jnp.float32)] * RANGES,
         *[pltpu.ACC(1)((ROWS, TILE), jnp.float32)] * RANGES,
-        pltpu.ACC(0)((owned, TILE), jnp.float32),
-        pltpu.ACC(1)((owned, TILE), jnp.float32))
+        *[pltpu.ACC(m % 2)((owned, TILE), jnp.float32) for m in range(4)])
 
     mark("valswait")
     bulk_wait(vals_in.at[pl.ds(0, n - 1)], vals_recv)

time: 24.6 us -> 23.5 us (0.955)
  Pallas kernels: 22.6 us -> 21.5 us
    pallas_call x1, Pallas kernels: 22.6 us -> 21.5 us  [fused_body(): pl.pallas_call(functools.partial(kernel, n, nf, rows_dev * n, capacity),...]
where the time goes in v3:
time: 23.5 us; the launch traced here: 23.3 us
  Pallas kernels  21.5 us (91%)
  local copies, waits for them, and re-layouts  1.12 us (5%)
  between operations  0.64 us (3%)
    pallas_call x1, Pallas kernels, fused_body(): pl.pallas_call(functools.partial(kernel, n, nf, rows_dev * n, capacity),...  21.5 us
    unnamed x2, local copies, waits for them, and re-layouts  1.12 us

profile of v3, /device:TPU:12, one launch (start us, length us, event | category | flops | bytes accessed | tf_op | source)
XLA Modules:
  0.0 23.3 jit_solution(16139355430717145512)
XLA Ops:
  0.6 21.5 %shard_map.59 = (f32[1,32]{1,0:T(1,128)S(1)}, f32[32,100]{1,0:T(8,128)S(1)}) custom-call(bf16[64,64]{1,0:T(8,128)(2,1)} %q_hbm.1, s32[1,1024]{1,0:T(1,128)} %bitcast.3, s32[32,100]{1,0:T(8,128)} %cand_hbm.1, bf16[16384,128]{1,0:T(8,128)(2,1)} %corpus_ref.1), custom_call_target="tpu_custom_call" | custom-call | tf_op jit(solution)/shard_map/pallas_call | solution.py:533
  22.2 0.5 %copy.8 = f32[32]{0:T(128)} copy(f32[32]{0:T(128)S(1)} %bitcast.2) | data formatting | bytes 256
  22.7 0.6 %copy.9 = f32[32,100]{1,0:T(8,128)} copy(f32[32,100]{1,0:T(8,128)S(1)} %get-tuple-element.7) | data formatting | bytes 25600

commit v4 on v3

--- a/solution.py
+++ b/solution.py
@@ -19,8 +19,8 @@
     0: (74, 32, (96, 112)), 1: (106, 22, (128, 144)), 2: (154, 32, (176, 192)),
 }
 PLAN = {
-    20: (("arrive", 1),),
-    38: (("mass", 0), ("reach", 2), ("hand", 1), ("reach", 3)),
+    20: (("arrive", 1), ("reach", 3)),
+    38: (("mass", 0), ("reach", 2), ("hand", 1)),
     54: (("ids", 0),),
     58: (("arrive", 2),),
     70: (("mass", 1), ("sm", 0)),

time: 23.5 us -> 23.2 us (0.987)
  Pallas kernels: 21.5 us -> 21.1 us
    pallas_call x1, Pallas kernels: 21.5 us -> 21.1 us  [fused_body(): pl.pallas_call(functools.partial(kernel, n, nf, rows_dev * n, capacity),...]
where the time goes in v4:
time: 23.2 us; the launch traced here: 22.9 us
  Pallas kernels  21.1 us (91%)
  local copies, waits for them, and re-layouts  1.12 us (5%)
  between operations  0.64 us (3%)
    pallas_call x1, Pallas kernels, fused_body(): pl.pallas_call(functools.partial(kernel, n, nf, rows_dev * n, capacity),...  21.1 us
    unnamed x2, local copies, waits for them, and re-layouts  1.12 us

profile of v4, /device:TPU:12, one launch (start us, length us, event | category | flops | bytes accessed | tf_op | source)
XLA Modules:
  0.0 22.9 jit_solution(8997125126529670528)
XLA Ops:
  0.6 21.1 %shard_map.59 = (f32[1,32]{1,0:T(1,128)S(1)}, f32[32,100]{1,0:T(8,128)S(1)}) custom-call(bf16[64,64]{1,0:T(8,128)(2,1)} %q_hbm.1, s32[1,1024]{1,0:T(1,128)} %bitcast.3, s32[32,100]{1,0:T(8,128)} %cand_hbm.1, bf16[16384,128]{1,0:T(8,128)(2,1)} %corpus_ref.1), custom_call_target="tpu_custom_call" | custom-call | tf_op jit(solution)/shard_map/pallas_call | solution.py:533
  21.8 0.5 %copy.8 = f32[32]{0:T(128)} copy(f32[32]{0:T(128)S(1)} %bitcast.2) | data formatting | bytes 256
  22.3 0.6 %copy.9 = f32[32,100]{1,0:T(8,128)} copy(f32[32,100]{1,0:T(8,128)S(1)} %get-tuple-element.7) | data formatting | bytes 25600
